TPU v7x, 32 devices: a whole 2x2x4 slice. The times are simulated.
32 devices in a mesh: row: 2 (over x), col: 16 (over z, y, core).
Axes of the slice: x: 2, y: 2, z: 4, core: 2. Of those that a mesh axis runs over, the one named last changes fastest.
Arguments:
- matrix: bfloat16 [1024, 65536], P('row', 'col'), may hold values from -0.1875 to 0.1875
- measured: float32 [256, 1024], P(None, 'row'), may hold values from -160 to 160
- support: int32 [4, 1024], replicated, may hold values from 0 to 65535, as said below
Outputs:
- estimate: float32 [256, 65536], P('row', 'col')
- row_norms: float32 [65536], P('col')
- residual_energy: float32 [4], replicated
Inputs may be any that keep to these rules, and one draw needn't show every extreme that they name: Each row of support lists 1024 distinct signal-row indices in increasing order; in every row, each aligned block of 4096 indices (the signal rows of one index of col) holds at most 128 of them, and some block exactly 128.
All inputs are finite; a program needn't handle non-finite values.
Results may differ from a plain program's by a relative error of at most 0.015.
Values may be sent and summed in bfloat16 or wider, within the bound.
A program may use at most 64 MiB of HBM per device.

v0:
```python
import jax
import jax.numpy as jnp
from jax import lax
from jax.sharding import PartitionSpec as P

KMAX = 128
STEP_SIZE = 0.25
HI = lax.Precision.HIGHEST
NT = (((1,), (1,)), ((), ()))


def window(support_row, start, width):
    below = jnp.sum((support_row < start).astype(jnp.int32))
    local = support_row - start
    inside = (local >= 0) & (local < width)
    slot = jnp.arange(support_row.shape[0]) - below
    chosen = (slot[None, :] == jnp.arange(KMAX)[:, None]) & inside[None, :]
    return jnp.sum(jnp.where(chosen, local[None, :] + 1, 0), axis=1) - 1


def local(matrix, measured, support):
    signals = measured.shape[0]
    n_row = lax.axis_size("row")
    rows_mine = signals // n_row
    columns = matrix.shape[1]
    offset = lax.axis_index("col") * columns
    iterations = support.shape[0]
    total_count = signals * measured.shape[1] * n_row
    lanes = jnp.arange(columns)
    index = [window(support[t], offset, columns) for t in range(iterations)]
    onehot = [(i[:, None] == lanes[None, :]).astype(jnp.bfloat16) for i in index]
    kept = [
        lax.dot_general(e, matrix, NT, preferred_element_type=jnp.float32).astype(jnp.bfloat16)
        for e in onehot[:-1]
    ]
    residual = measured
    current = jnp.zeros((signals, KMAX), jnp.float32)
    energies = []
    for t in range(iterations):
        energies.append(jnp.sum(residual * residual))
        half = residual.astype(jnp.bfloat16)
        if t == iterations - 1:
            break
        part = lax.dot_general(half, kept[t], NT, preferred_element_type=jnp.float32)
        gradient = lax.psum(part.astype(jnp.bfloat16), "row").astype(jnp.float32)
        if t:
            same = (index[t - 1][:, None] == index[t][None, :]) & (index[t] >= 0)[None, :]
            current = jnp.dot(current, same.astype(jnp.float32), precision=HI)
        current = current + STEP_SIZE * gradient
        image = jnp.dot(current.astype(jnp.bfloat16), kept[t], preferred_element_type=jnp.float32)
        residual = measured - lax.psum(image.astype(jnp.bfloat16), "col").astype(jnp.float32)
    gradient = lax.psum_scatter(
        jnp.dot(half, matrix, preferred_element_type=jnp.float32).astype(jnp.bfloat16),
        "row",
        scatter_dimension=0,
        tiled=True,
    ).astype(jnp.float32)
    mine = lax.dynamic_slice_in_dim(current, lax.axis_index("row") * rows_mine, rows_mine, 0)
    stepped = jnp.dot(mine, onehot[-2].astype(jnp.float32), precision=HI) + STEP_SIZE * gradient
    keep = jnp.sum(onehot[-1].astype(jnp.float32), axis=0)
    sums = jnp.concatenate([jnp.sum(stepped * stepped, axis=0), jnp.stack(energies)])
    sums = lax.psum(sums, "row")
    return (stepped * keep[None, :], jnp.sqrt(sums[:columns]), sums[columns:] / total_count)


def solution(mesh):
    placed = (P("row", "col"), P(None, "row"), P())
    return jax.shard_map(
        local,
        mesh=mesh,
        in_specs=placed,
        out_specs=(P("row", "col"), P("col"), P()),
        check_vma=False,
    )
```

profile of v0, /device:TPU:0, one launch (start us, length us, event | category | flops | bytes accessed | tf_op | source)
XLA Modules:
  0.0 428.1 jit_solution(17295335813921915850)
XLA Ops:
  7.2 0.0 all-reduce.7.cloned.1.call-start
  7.2 0.9 and_reduce_fusion
  8.2 1.6 subtract_add_fusion
  9.8 1.3 iota_subtract_fusion.2
  11.1 0.2 select_reduce_fusion.3
  11.3 3.8 fusion.5
  15.0 0.9 fusion.7
  15.9 0.0 all-reduce.7.cloned.1.call-update
  15.9 0.0 all-reduce.9.cloned.1.call-start
  16.0 0.2 select_reduce_fusion.2
  16.2 3.7 fusion.4
  19.9 19.9 %all-reduce.7.cloned.1.call-done = bf16[256,128]{0,1:T(8,128)(2,1)} async-done(((bf16[256,128]{0,1:T(8,128)(2,1)}), bf16[256,128]{0,1:T(8,128)(2,1)}) %all-reduce.7.cloned.1.call-update) | async-done | bytes 65552 | tf_op jit(solution)/shard_map/psum | solution.py:45
  39.8 1.8 convolution_convert_fusion.3
  41.5 0.0 all-reduce.9.cloned.1.call-update
  41.6 0.0 all-reduce.11.cloned.1.call-start
  41.6 1.3 iota_subtract_fusion
  42.9 0.2 select_reduce_fusion.1
  43.1 90.4 %all-reduce.9.cloned.1.call-done = bf16[256,512]{1,0:T(8,128)(2,1)} async-done(((bf16[256,512]{1,0:T(8,128)(2,1)}), bf16[256,512]{1,0:T(8,128)(2,1)}) %all-reduce.9.cloned.1.call-update) | async-done | bytes 262160 | tf_op jit(solution)/shard_map/psum | solution.py:51
  133.4 1.8 convolution_convert_fusion.5
  135.3 0.0 all-reduce.13.cloned.1.call-start
  135.3 22.4 %all-reduce.11.cloned.1.call-done = bf16[256,128]{0,1:T(8,128)(2,1)} async-done(((bf16[256,128]{0,1:T(8,128)(2,1)}), bf16[256,128]{0,1:T(8,128)(2,1)}) %all-reduce.11.cloned.1.call-update) | async-done | bytes 65552 | tf_op jit(solution)/shard_map/psum | solution.py:45
  157.7 1.2 convolution_add_fusion.2
  158.9 1.0 convolution_convert_fusion.2
  159.9 0.0 all-reduce.13.cloned.1.call-update
  159.9 0.0 all-reduce.15.cloned.1.call-start
  160.0 3.7 fusion.6
  163.7 87.6 %all-reduce.13.cloned.1.call-done = bf16[256,512]{1,0:T(8,128)(2,1)} async-done(((bf16[256,512]{1,0:T(8,128)(2,1)}), bf16[256,512]{1,0:T(8,128)(2,1)}) %all-reduce.13.cloned.1.call-update) | async-done | bytes 262160 | tf_op jit(solution)/shard_map/psum | solution.py:51
  251.3 1.8 convolution_convert_fusion.4
  253.1 0.0 all-reduce.15.cloned.1.call-update
  253.1 0.0 all-reduce.17.cloned.1.call-start
  253.2 22.2 %all-reduce.15.cloned.1.call-done = bf16[256,128]{0,1:T(8,128)(2,1)} async-done(((bf16[256,128]{0,1:T(8,128)(2,1)}), bf16[256,128]{0,1:T(8,128)(2,1)}) %all-reduce.15.cloned.1.call-update) | async-done | bytes 65552 | tf_op jit(solution)/shard_map/psum | solution.py:45
  275.4 1.2 convolution_add_fusion.1
  276.6 1.0 convolution_convert_fusion.1
  277.5 0.0 reduce-scatter.2.cloned.1.call-start
  277.6 91.3 %all-reduce.17.cloned.1.call-done = bf16[256,512]{1,0:T(8,128)(2,1)} async-done(((bf16[256,512]{1,0:T(8,128)(2,1)}), bf16[256,512]{1,0:T(8,128)(2,1)}) %all-reduce.17.cloned.1.call-update) | async-done | bytes 262160 | tf_op jit(solution)/shard_map/psum | solution.py:51
  368.9 4.9 %convolution_convert_fusion = bf16[256,4096]{1,0:T(8,128)(2,1)} fusion(bf16[512,4096]{1,0:T(8,128)(2,1)} %param.3, f32[256,512]{1,0:T(8,128)S(1)} %copy-done, bf16[256,512]{1,0:T(8,128)(2,1)} %all-reduce.17.cloned.1.call-done), kind=kOutput, calls=%fused_computation | convolution fusion | flops 1075183616 | bytes 7077888 | tf_op jit(solution)/shard_map/dot_general | solution.py:53
  373.8 0.2 select_reduce_fusion
  374.0 0.3 convert_reduce_fusion
  374.3 0.4 copy-done.1
  374.7 0.1 copy-done.2
  374.8 0.1 copy-done.3
  374.9 0.9 multiply_reduce_fusion.1
  375.8 30.5 %reduce-scatter.2.cloned.1.call-done = bf16[128,4096]{1,0:T(8,128)(2,1)} async-done(((bf16[256,4096]{1,0:T(8,128)(2,1)}), bf16[128,4096]{1,0:T(8,128)(2,1)}) %reduce-scatter.2.cloned.1.call-update) | async-done | bytes 1048592 | tf_op jit(solution)/shard_map/reduce_scatter | solution.py:52
  406.4 4.1 multiply_reduce_fusion
  410.4 2.6 concatenate.3
  413.1 7.1 %psum.55 = f32[4100]{0:T(1024)S(1)} all-reduce(f32[4100]{0:T(1024)S(1)} %concatenate.3), channel_id=1, replica_groups=mesh['row'=2,'col'=16] {'row'}, use_global_device_ids=true, to_apply=%region_21.22 | all-reduce | flops 4100 | bytes 32800 | tf_op jit(solution)/shard_map/psum | solution.py:62
  420.2 0.5 slice_multiply_fusion
  420.7 0.6 slice_sqrt_fusion
  (14 shorter events, 0.1 us)
Async XLA Ops:
  7.2 32.6 %all-reduce.7.cloned.1.call-start = ((), (), s32[]{:S(2)}) async-start(), calls=%async_computation.1 | async-start | bytes 131072 | tf_op jit(solution)/shard_map/psum | solution.py:45
  11.3 3.8 copy-start
  15.9 117.5 %all-reduce.9.cloned.1.call-start = ((), (), s32[]{:S(2)}) async-start(), calls=%async_computation.2 | async-start | bytes 524288 | tf_op jit(solution)/shard_map/psum | solution.py:51
  41.6 116.1 %all-reduce.11.cloned.1.call-start = ((), (), s32[]{:S(2)}) async-start(), calls=%async_computation.3 | async-start | bytes 131072 | tf_op jit(solution)/shard_map/psum | solution.py:45
  135.3 116.0 %all-reduce.13.cloned.1.call-start = ((), (), s32[]{:S(2)}) async-start(), calls=%async_computation.4 | async-start | bytes 524288 | tf_op jit(solution)/shard_map/psum | solution.py:51
  159.9 115.5 %all-reduce.15.cloned.1.call-start = ((), (), s32[]{:S(2)}) async-start(), calls=%async_computation.5 | async-start | bytes 131072 | tf_op jit(solution)/shard_map/psum | solution.py:45
  253.1 115.8 %all-reduce.17.cloned.1.call-start = ((), (), s32[]{:S(2)}) async-start(), calls=%async_computation.6 | async-start | bytes 524288 | tf_op jit(solution)/shard_map/psum | solution.py:51
  277.5 128.8 %reduce-scatter.2.cloned.1.call-start = ((), (), s32[]{:S(2)}) async-start(), calls=%async_computation.7 | async-start | bytes 3145728 | tf_op jit(solution)/shard_map/reduce_scatter | solution.py:52
  373.8 0.9 copy-start.1
  373.8 1.0 copy-start.2
  373.8 1.1 copy-start.3
Sparse Core Ops, SparseCore 0:
  16.0 23.6 all-reduce.6
  43.7 89.6 all-reduce.8
  136.3 21.4 all-reduce.10
  161.5 89.6 all-reduce.12
  253.9 21.4 all-reduce.14
  279.2 89.6 all-reduce.16
  373.9 32.3 reduce-scatter.1
where the time goes:
time: 429 us; the launch traced here: 428 us
  waiting for transfers between devices  364 us (85%)
  matrix products  30.6 us (7%)
  between operations  14.2 us (3%)
  other arithmetic  7.66 us (2%)
  blocking collectives  7.1 us (2%)
    psum x3, waiting for transfers between devices, local(): lax.psum(image.astype(jnp.bfloat16), 'col').astype(jnp.float32)  269 us
    psum x3, waiting for transfers between devices, local(): gradient = lax.psum(part.astype(jnp.bfloat16), 'row').astype(jnp.float32)  64.5 us
    reduce_scatter x1, waiting for transfers between devices, local(): lax.psum_scatter(jnp.dot(half, matrix, preferred_element_type=jnp.float32...  30.5 us
    dot_general x3, matrix products, local(): lax.dot_general(e, matrix, NT, preferred_element_type=jnp.float32)  11.1 us
  transfers between devices with their start and end apart: 7, of which 7 were waited for; matrix products, arithmetic and copies ran while one was open for 2% of the time, Pallas kernels for 0%

commit v1 on v0

--- a/solution.py
+++ b/solution.py
@@ -7,6 +7,12 @@
 STEP_SIZE = 0.25
 HI = lax.Precision.HIGHEST
 NT = (((1,), (1,)), ((), ()))
+
+
+def summed_here(x, axis):
+    shards = lax.all_gather(x, axis, axis=0, tiled=False)
+    total = shards.sum(axis=0)
+    return total
 
 
 def window(support_row, start, width):
@@ -42,7 +48,7 @@
         if t == iterations - 1:
             break
         part = lax.dot_general(half, kept[t], NT, preferred_element_type=jnp.float32)
-        gradient = lax.psum(part.astype(jnp.bfloat16), "row").astype(jnp.float32)
+        gradient = summed_here(part.astype(jnp.bfloat16), "row").astype(jnp.float32)
         if t:
             same = (index[t - 1][:, None] == index[t][None, :]) & (index[t] >= 0)[None, :]
             current = jnp.dot(current, same.astype(jnp.float32), precision=HI)

time: 429 us -> 369 us (0.86)
  waiting for transfers between devices: 364 us -> 295 us
  blocking collectives: 7.1 us -> 23.2 us
  matrix products: 30.6 us -> 23.9 us
    psum x3 -> x0, waiting for transfers between devices: 64.5 us -> none  [local(): gradient = lax.psum(part.astype(jnp.bfloat16), 'row').astype(jnp.float32)]
    all_gather x0 -> x3, blocking collectives: none -> 16.1 us  [summed_here(): shards = lax.all_gather(x, axis, axis=0, tiled=False)]
    psum x3, waiting for transfers between devices: 269 us -> 265 us  [local(): lax.psum(image.astype(jnp.bfloat16), 'col').astype(jnp.float32)]
  transfers between devices with their start and end apart: 7 -> 4, of which waited for: 7 -> 4; matrix products, arithmetic and copies ran while one was open for 2% -> 2% of each run, Pallas kernels for 0% -> 0%
where the time goes in v1:
time: 369 us
  waiting for transfers between devices  295 us (80%)
  matrix products  23.9 us (6%)
  blocking collectives  23.2 us (6%)
  between operations  13.9 us (4%)
  other arithmetic  8.19 us (2%)
  local copies, waits for them, and re-layouts  3.96 us (1%)
    psum x3, waiting for transfers between devices, local(): lax.psum(image.astype(jnp.bfloat16), 'col').astype(jnp.float32)  265 us
    reduce_scatter x1, waiting for transfers between devices, local(): lax.psum_scatter(jnp.dot(half, matrix, preferred_element_type=jnp.float32...  30.5 us
    all_gather x3, blocking collectives, summed_here(): shards = lax.all_gather(x, axis, axis=0, tiled=False)  16.1 us
    dot_general x3, matrix products, local(): lax.dot_general(e, matrix, NT, preferred_element_type=jnp.float32)  9.09 us
  transfers between devices with their start and end apart: 4, of which 4 were waited for; matrix products, arithmetic and copies ran while one was open for 2% of the time, Pallas kernels for 0%

profile of v1, /device:TPU:0, one launch (start us, length us, event | category | flops | bytes accessed | tf_op | source)
XLA Modules:
  0.0 368.8 jit_solution(1508874714919351130)
XLA Ops:
  7.2 0.0 all-reduce.4.cloned.1.call-start
  7.2 0.9 and_reduce_fusion
  8.2 1.7 subtract_add_fusion
  9.8 1.3 iota_subtract_fusion.2
  11.1 0.2 select_reduce_fusion.3
  11.3 3.8 %fusion.5 = bf16[128,512]{1,0:T(8,128)(2,1)S(1)} fusion(bf16[512,4096]{1,0:T(8,128)(2,1)} %param.3, s32[128]{0:T(128)S(1)} %broadcast_add_fusion.3), kind=kOutput, calls=%fused_computation.16 | convolution fusion | flops 537460736 | bytes 4325888 | tf_op jit(solution)/shard_map/dot_general | solution.py:39
  15.1 0.0 copy-done
  15.1 0.2 fusion.7
  15.3 5.9 %all-gather = bf16[512,128]{0,1:T(8,128)(2,1)S(1)} all-gather(bf16[256,128]{0,1:T(8,128)(2,1)S(1)} %fusion.7), channel_id=2, replica_groups=mesh['row'=2,'col'=16] {'row'}, dimensions={0}, use_global_device_ids=true | all-gather | bytes 196608 | tf_op jit(solution)/shard_map/all_gather | solution.py:13
  21.2 0.3 reduce_sum.164
  21.5 0.1 copy.7
  21.7 0.9 convolution_convert_fusion.3
  22.6 0.0 all-reduce.4.cloned.1.call-update
  22.6 0.0 all-reduce.6.cloned.1.call-start
  22.7 0.2 select_reduce_fusion.2
  22.9 1.3 iota_subtract_fusion
  24.2 0.2 select_reduce_fusion.1
  24.4 3.8 %fusion.6 = bf16[128,512]{1,0:T(8,128)(2,1)S(1)} fusion(bf16[512,4096]{1,0:T(8,128)(2,1)} %param.3, s32[128]{0:T(128)S(1)} %broadcast_add_fusion.1), kind=kOutput, calls=%fused_computation.17 | convolution fusion | flops 537460736 | bytes 4325888 | tf_op jit(solution)/shard_map/dot_general | solution.py:39
  28.3 1.5 fusion.4
  29.8 84.5 %all-reduce.4.cloned.1.call-done = bf16[256,512]{1,0:T(8,128)(2,1)} async-done(((bf16[256,512]{1,0:T(8,128)(2,1)}), bf16[256,512]{1,0:T(8,128)(2,1)}) %all-reduce.4.cloned.1.call-update) | async-done | bytes 262160 | tf_op jit(solution)/shard_map/psum | solution.py:57
  114.3 1.2 convolution_convert_fusion.5
  115.5 5.1 %all-gather.1 = bf16[512,128]{1,0:T(8,128)(2,1)S(1)} all-gather(bf16[256,128]{1,0:T(8,128)(2,1)S(1)} %convolution_convert_fusion.5), channel_id=3, replica_groups=mesh['row'=2,'col'=16] {'row'}, dimensions={0}, use_global_device_ids=true | all-gather | bytes 196608 | tf_op jit(solution)/shard_map/all_gather | solution.py:13
  120.6 0.3 convolution_add_fusion.2
  120.9 0.9 convolution_convert_fusion.2
  121.8 0.0 all-reduce.6.cloned.1.call-update
  121.8 0.0 all-reduce.8.cloned.1.call-start
  121.9 90.2 %all-reduce.6.cloned.1.call-done = bf16[256,512]{1,0:T(8,128)(2,1)} async-done(((bf16[256,512]{1,0:T(8,128)(2,1)}), bf16[256,512]{1,0:T(8,128)(2,1)}) %all-reduce.6.cloned.1.call-update) | async-done | bytes 262160 | tf_op jit(solution)/shard_map/psum | solution.py:57
  212.1 1.2 convolution_convert_fusion.4
  213.2 5.1 %all-gather.2 = bf16[512,128]{1,0:T(8,128)(2,1)S(1)} all-gather(bf16[256,128]{1,0:T(8,128)(2,1)S(1)} %convolution_convert_fusion.4), channel_id=4, replica_groups=mesh['row'=2,'col'=16] {'row'}, dimensions={0}, use_global_device_ids=true | all-gather | bytes 196608 | tf_op jit(solution)/shard_map/all_gather | solution.py:13
  218.4 0.3 convolution_add_fusion.1
  218.7 0.9 convolution_convert_fusion.1
  219.6 0.0 all-reduce.8.cloned.1.call-update
  219.6 0.0 reduce-scatter.2.cloned.1.call-start
  219.6 90.2 %all-reduce.8.cloned.1.call-done = bf16[256,512]{1,0:T(8,128)(2,1)} async-done(((bf16[256,512]{1,0:T(8,128)(2,1)}), bf16[256,512]{1,0:T(8,128)(2,1)}) %all-reduce.8.cloned.1.call-update) | async-done | bytes 262160 | tf_op jit(solution)/shard_map/psum | solution.py:57
  309.8 4.9 %convolution_convert_fusion = bf16[256,4096]{1,0:T(8,128)(2,1)} fusion(bf16[512,4096]{1,0:T(8,128)(2,1)} %param.3, f32[256,512]{1,0:T(8,128)S(1)} %copy-done, bf16[256,512]{1,0:T(8,128)(2,1)} %all-reduce.8.cloned.1.call-done), kind=kOutput, calls=%fused_computation | convolution fusion | flops 1075183616 | bytes 7077888 | tf_op jit(solution)/shard_map/dot_general | solution.py:59
  314.7 0.0 reduce-scatter.2.cloned.1.call-update
  314.7 0.2 select_reduce_fusion
  314.9 0.3 convert_reduce_fusion
  315.3 0.4 copy-done.1
  315.7 0.1 copy-done.2
  315.7 0.1 copy-done.3
  315.8 1.0 multiply_reduce_fusion.1
  316.8 30.5 %reduce-scatter.2.cloned.1.call-done = bf16[128,4096]{1,0:T(8,128)(2,1)} async-done(((bf16[256,4096]{1,0:T(8,128)(2,1)}), bf16[128,4096]{1,0:T(8,128)(2,1)}) %reduce-scatter.2.cloned.1.call-update) | async-done | bytes 1048592 | tf_op jit(solution)/shard_map/reduce_scatter | solution.py:58
  347.3 4.1 %multiply_reduce_fusion = (f32[4096]{0:T(1024)S(1)}, f32[128,4096]{1,0:T(8,128)}) fusion(f32[4096]{0:T(1024)S(1)} %convert_reduce_fusion, bf16[128,4096]{1,0:T(8,128)(2,1)} %reduce-scatter.2.cloned.1.call-done, s32[128]{0:T(128)S(1)} %broadcast_add_fusion.1, f32[256,128]{1,0:T(8,128)S(1)} %convolution_add_fusion.1, s32[]{:T(128)S(6)} %select_n.19), kind=kOutput, calls=%fused_computation.2 | convolution fusion | flops 808972288 | bytes 3244548 | tf_op jit(solution)/shard_map/dot_general | solution.py:65
  351.4 2.6 concatenate.3
  354.0 7.1 %psum.31 = f32[4100]{0:T(1024)S(1)} all-reduce(f32[4100]{0:T(1024)S(1)} %concatenate.3), channel_id=1, replica_groups=mesh['row'=2,'col'=16] {'row'}, use_global_device_ids=true, to_apply=%region_21.22 | all-reduce | flops 4100 | bytes 32800 | tf_op jit(solution)/shard_map/psum | solution.py:68
  361.1 0.5 slice_multiply_fusion
  361.6 0.6 slice_sqrt_fusion
  (15 shorter events, 0.1 us)
Async XLA Ops:
  7.2 107.1 %all-reduce.4.cloned.1.call-start = ((), (), s32[]{:S(2)}) async-start(), calls=%async_computation.1 | async-start | bytes 524288 | tf_op jit(solution)/shard_map/psum | solution.py:57
  11.3 3.8 %copy-start = (f32[256,512]{1,0:T(8,128)S(1)}, f32[256,512]{1,0:T(8,128)}, u32[]{:S(2)}) copy-start(f32[256,512]{1,0:T(8,128)} %param.4) | copy-start | bytes 1572868
  22.6 189.5 %all-reduce.6.cloned.1.call-start = ((), (), s32[]{:S(2)}) async-start(), calls=%async_computation.2 | async-start | bytes 524288 | tf_op jit(solution)/shard_map/psum | solution.py:57
  24.4 3.9 %copy-start.4 = (bf16[512,4096]{1,0:T(8,128)(2,1)S(1)}, bf16[512,4096]{1,0:T(8,128)(2,1)}, u32[]{:S(2)}) copy-start(bf16[512,4096]{1,0:T(8,128)(2,1)} %param.3) | copy-start | bytes 12582916
  121.8 188.0 %all-reduce.8.cloned.1.call-start = ((), (), s32[]{:S(2)}) async-start(), calls=%async_computation.3 | async-start | bytes 524288 | tf_op jit(solution)/shard_map/psum | solution.py:57
  219.6 127.7 %reduce-scatter.2.cloned.1.call-start = ((), (), s32[]{:S(2)}) async-start(), calls=%async_computation.4 | async-start | bytes 3145728 | tf_op jit(solution)/shard_map/reduce_scatter | solution.py:58
  314.7 0.9 copy-start.1
  314.7 1.0 copy-start.2
  314.7 1.1 copy-start.3
Sparse Core Ops, SparseCore 0:
  22.7 91.5 all-reduce.3
  122.0 90.0 all-reduce.5
  219.7 90.0 all-reduce.7
  314.9 32.3 reduce-scatter.1
